TPU v7x, 32 devices: a whole 2x2x4 slice. The times are simulated.
32 devices in a mesh: gx: 4 (over y, x), gy: 8 (over z, core).
Axes of the slice: x: 2, y: 2, z: 4, core: 2. Of those that a mesh axis runs over, the one named last changes fastest.
Arguments:
- replay_deter: float32 [8192, 2048], P(('gx', 'gy')), may hold values from -1 to 1
- replay_stoch: int32 [8192, 32], P(('gx', 'gy')), may hold values from 0 to 31
- send_rows: int32 [1024, 8], P(('gx', 'gy')), may hold values from 0 to 255
- send_counts: int32 [32, 32], P(('gx', 'gy')), may hold values from 0 to 8, as said below
- actions: int32 [8192, 4], P(('gx', 'gy')), may hold values from 0 to 17
- samples: int32 [8192, 4, 32], P(('gx', 'gy')), may hold values from 0 to 31
- w_stoch: bfloat16 [1024, 6144], P('gy'), may hold values from -1 to 1
- w_deter: bfloat16 [4, 512, 1536], P(None, 'gy'), may hold values from -0.25 to 0.25
- act_table: bfloat16 [18, 6144], replicated, may hold values from -3 to 3
- w_prior: bfloat16 [2048, 1024], P('gy'), may hold values from -0.037353516 to 0.037353516
Outputs:
- imagined: bfloat16 [8192, 4, 2048], P(('gx', 'gy'))
- log_prob: float32 [8192, 4, 32], P(('gx', 'gy'))
Inputs may be any that keep to these rules, and one draw needn't show every extreme that they name: `send_rows`: entries past a destination's count are unused. `send_counts`: each source's counts sum to exactly 128; every source sends 8 rows to some owner, and some owner receives 8 rows from every source.
All inputs are finite; a program needn't handle non-finite values.
Results may differ from a plain program's by a relative error of at most 0.0022.
Values may be sent and summed in bfloat16 or wider, within the bound.
No kernel may reach another device: no remote copies, remote signals or barrier semaphores. Data moves between devices by JAX's collectives and lax.ppermute only.
A program may use at most 128 MiB of HBM per device.

v0:
```python
import jax
import jax.numpy as jnp
from jax import lax
from jax.sharding import PartitionSpec as P

GROUPS = 32
CLASSES = 32
STEPS = 4


def gate_inputs(stoch, action, actions_count):
    rows = stoch.shape[0]
    onehot = (
        (stoch[:, :, None] == jnp.arange(CLASSES, dtype=jnp.int32)[None, None, :])
        .reshape(rows, GROUPS * CLASSES)
        .astype(jnp.bfloat16)
    )
    act_hot = (action[:, None] == jnp.arange(actions_count, dtype=jnp.int32)[None, :]).astype(
        jnp.bfloat16
    )
    return (onehot, act_hot)


def imagine(start, first, acts, samps, stoch_full, deter_full, act_table):
    blocks = deter_full.shape[0]
    width = deter_full.shape[1]
    pieces = [start[:, b * width : (b + 1) * width] for b in range(blocks)]
    stoch = first
    states = []
    for step in range(STEPS):
        onehot, act_hot = gate_inputs(stoch, acts[:, step], act_table.shape[0])
        input_term = jnp.dot(onehot, stoch_full, preferred_element_type=jnp.float32) + jnp.dot(
            act_hot, act_table, preferred_element_type=jnp.float32
        )
        fresh = []
        for b in range(blocks):
            before = pieces[b]
            gates = input_term[:, 3 * width * b : 3 * width * (b + 1)] + jnp.dot(
                before.astype(jnp.bfloat16), deter_full[b], preferred_element_type=jnp.float32
            )
            reset = jax.nn.sigmoid(gates[:, :width])
            cand = jnp.tanh(reset * gates[:, width : 2 * width])
            update = jax.nn.sigmoid(gates[:, 2 * width :] - 1.0)
            fresh.append(update * cand + (1.0 - update) * before)
        pieces = fresh
        states.append(jnp.concatenate(pieces, 1).astype(jnp.bfloat16))
        stoch = samps[:, step]
    return jnp.stack(states, 1)


def on_device(
    replay_deter,
    replay_stoch,
    send_rows,
    send_counts,
    actions,
    samples,
    w_stoch,
    w_deter,
    act_table,
    w_prior,
):
    peers, cap = send_rows.shape
    slots = peers * cap
    deter = replay_deter.shape[1]
    stoch_full = lax.all_gather(w_stoch, "gy", axis=0, tiled=True)
    deter_full = lax.all_gather(w_deter, "gy", axis=1, tiled=True)
    outgoing = (jnp.arange(cap, dtype=jnp.int32)[None, :] < send_counts[0][:, None]).astype(
        jnp.int32
    )
    start = replay_deter[send_rows]
    first = replay_stoch[send_rows]
    start, first, live = (
        lax.all_to_all(start, ("gx", "gy"), split_axis=0, concat_axis=0, tiled=True),
        lax.all_to_all(first, ("gx", "gy"), split_axis=0, concat_axis=0, tiled=True),
        lax.all_to_all(outgoing, ("gx", "gy"), split_axis=0, concat_axis=0, tiled=True),
    )
    live = live.reshape(slots)
    states = imagine(
        start.reshape(slots, deter),
        first.reshape(slots, GROUPS),
        actions,
        samples,
        stoch_full,
        deter_full,
        act_table,
    )
    states = jnp.where(live[:, None, None] > 0, states, jnp.zeros_like(states))
    prior_full = lax.all_gather(w_prior, "gy", axis=0, tiled=True)
    logits = jnp.dot(
        states.reshape(slots * STEPS, deter), prior_full, preferred_element_type=jnp.float32
    )
    logits = logits.reshape(slots, STEPS, GROUPS, CLASSES)
    totals = jnp.log(jnp.sum(jnp.exp(logits), -1))
    hits = samples[..., None] == jnp.arange(CLASSES, dtype=jnp.int32)
    picked = jnp.sum(jnp.where(hits, logits, jnp.zeros_like(logits)), -1)
    log_prob = jnp.where(live[:, None, None] > 0, picked - totals, jnp.zeros_like(totals))
    return (states, log_prob)


def solution(mesh):
    in_specs = (
        P(("gx", "gy"), None),
        P(("gx", "gy"), None),
        P(("gx", "gy"), None),
        P(("gx", "gy"), None),
        P(("gx", "gy"), None),
        P(("gx", "gy"), None, None),
        P("gy", None),
        P(None, "gy", None),
        P(),
        P("gy", None),
    )
    out_specs = (P(("gx", "gy"), None, None), P(("gx", "gy"), None, None))
    return jax.shard_map(
        on_device, mesh=mesh, in_specs=in_specs, out_specs=out_specs, check_vma=False
    )
```

profile of v0, /device:TPU:0, one launch (start us, length us, event | category | flops | bytes accessed | tf_op | source)
XLA Modules:
  0.0 338.7 jit_solution(16087413320578995944)
XLA Ops:
  10.8 7.3 %all-to-all-start = ((s32[32,1,8]{2,1,0:T(1,128)}), s32[32,1,8]{2,1,0:T(1,128)S(1)}, u32[]{:S(2)}, u32[]{:S(2)}) async-start(s32[32,1,8]{2,1,0:T(1,128)} %compare_convert_fusion), calls=%async_computation | async-start | bytes 32768 | tf_op jit(solution)/shard_map/all_to_all | solution.py:76
  21.3 3.9 %all-to-all-done = s32[32,1,8]{2,1,0:T(1,128)S(1)} async-done(((s32[32,1,8]{2,1,0:T(1,128)}), s32[32,1,8]{2,1,0:T(1,128)S(1)}, u32[]{:S(2)}, u32[]{:S(2)}) %all-to-all-start) | async-done | bytes 1056 | tf_op jit(solution)/shard_map/all_to_all | solution.py:76
  25.2 2.6 all-to-all-start.1
  27.8 2.7 gather_fusion.1
  30.5 5.0 %all-to-all-done.1 = s32[32,1,256]{2,1,0:T(1,128)S(1)} async-done(((s32[32,1,256]{2,1,0:T(1,128)}), s32[32,1,256]{2,1,0:T(1,128)S(1)}, u32[]{:S(2)}, u32[]{:S(2)}) %all-to-all-start.1) | async-done | bytes 32800 | tf_op jit(solution)/shard_map/all_to_all | solution.py:75
  35.4 2.7 all-to-all-start.2
  41.3 41.9 %all-gather.8.cloned.1.call-done = bf16[2048,1024]{1,0:T(8,128)(2,1)} async-done(((bf16[256,1024]{1,0:T(8,128)(2,1)}), bf16[2048,1024]{1,0:T(8,128)(2,1)}) %all-gather.8.cloned.1.call-update) | async-done | bytes 4194320 | tf_op jit(solution)/shard_map/all_gather | solution.py:89
  83.2 6.5 %copy.26 = bf16[1024,2048]{1,0:T(8,128)(2,1)} copy(bf16[1024,2048]{0,1:T(8,128)(2,1)} %bitcast.116) | data formatting | bytes 8388608 | tf_op jit(solution)/shard_map/dot_general | solution.py:90
  89.7 116.9 %all-gather.4.cloned.1.call-done = bf16[1024,6144]{1,0:T(8,128)(2,1)} async-done(((bf16[128,6144]{1,0:T(8,128)(2,1)}), bf16[1024,6144]{1,0:T(8,128)(2,1)}) %all-gather.4.cloned.1.call-update) | async-done | bytes 12582928 | tf_op jit(solution)/shard_map/all_gather | solution.py:66
  206.6 7.0 %fusion.199 = f32[256,6144]{1,0:T(8,128)S(1)} fusion(pred[256,1024]{0,1:T(32,128)(4,1)S(1)} %get-tuple-element.50, bf16[1024,6144]{1,0:T(8,128)(2,1)} %all-gather.4.cloned.1.call-done), kind=kOutput, calls=%fused_computation.297 | convolution fusion | flops 3221225472 | bytes 19136512 | tf_op jit(solution)/shard_map/dot_general | solution.py:32
  213.6 3.7 %convolution_add_fusion.3 = f32[256,6144]{1,0:T(8,128)} fusion(f32[256,6144]{1,0:T(8,128)S(1)} %fusion.199, bf16[18,6144]{1,0:T(8,128)(2,1)S(1)} %copy-done.3, s32[256]{0:T(256)S(1)} %bitcast.122), kind=kOutput, calls=%fused_computation.5 | convolution fusion | flops 58200576 | bytes 12805120 | tf_op jit(solution)/shard_map/dot_general | solution.py:32
  217.3 3.6 %fusion.200 = f32[256,6144]{1,0:T(8,128)S(1)} fusion(pred[256,1024]{0,1:T(32,128)(4,1)S(1)} %get-tuple-element.48, bf16[1024,6144]{1,0:T(8,128)(2,1)S(1)} %bitcast.104), kind=kOutput, calls=%fused_computation.298 | convolution fusion | flops 3221225472 | bytes 19136512 | tf_op jit(solution)/shard_map/dot_general | solution.py:32
  221.0 3.6 %convolution_add_fusion.2 = f32[256,6144]{1,0:T(8,128)} fusion(f32[256,6144]{1,0:T(8,128)S(1)} %fusion.200, bf16[18,6144]{1,0:T(8,128)(2,1)S(1)} %copy-done.3, s32[256]{0:T(256)S(1)} %bitcast.121), kind=kOutput, calls=%fused_computation.4 | convolution fusion | flops 58200576 | bytes 12805120 | tf_op jit(solution)/shard_map/dot_general | solution.py:32
  224.6 47.0 %all-gather.6.cloned.1.call-done = bf16[4,512,1536]{2,1,0:T(8,128)(2,1)} async-done(((bf16[4,64,1536]{2,1,0:T(8,128)(2,1)}), bf16[4,512,1536]{2,1,0:T(8,128)(2,1)}) %all-gather.6.cloned.1.call-update) | async-done | bytes 6291472 | tf_op jit(solution)/shard_map/all_gather | solution.py:67
  271.6 2.6 convolution_add_fusion.16
  274.2 2.6 convolution_add_fusion.17
  278.8 2.1 convolution_add_fusion.19
  281.0 2.3 convert_bitcast_fusion.11
  287.9 5.6 %fusion.201 = f32[256,6144]{1,0:T(8,128)} fusion(pred[256,1024]{0,1:T(32,128)(4,1)S(1)} %copy-done.14, bf16[1024,6144]{1,0:T(8,128)(2,1)S(1)} %bitcast.106), kind=kOutput, calls=%fused_computation.299 | convolution fusion | flops 3221225472 | bytes 19136512 | tf_op jit(solution)/shard_map/dot_general | solution.py:32
  293.5 3.8 %convolution_add_fusion.1 = f32[256,6144]{1,0:T(8,128)S(1)} fusion(f32[256,6144]{1,0:T(8,128)} %fusion.201, bf16[18,6144]{1,0:T(8,128)(2,1)S(1)} %copy-done.4, s32[256]{0:T(256)S(1)} %bitcast.120), kind=kOutput, calls=%fused_computation.3 | convolution fusion | flops 58200576 | bytes 12805120 | tf_op jit(solution)/shard_map/dot_general | solution.py:32
  299.2 6.5 %fusion.202 = f32[256,6144]{1,0:T(8,128)} fusion(pred[256,1024]{0,1:T(32,128)(4,1)} %get-tuple-element.47, bf16[1024,6144]{1,0:T(8,128)(2,1)S(1)} %bitcast.106), kind=kOutput, calls=%fused_computation.300 | convolution fusion | flops 3221225472 | bytes 19136512 | tf_op jit(solution)/shard_map/dot_general | solution.py:32
  305.7 3.9 %convolution_add_fusion = f32[256,6144]{1,0:T(8,128)S(1)} fusion(f32[256,6144]{1,0:T(8,128)} %fusion.202, bf16[18,6144]{1,0:T(8,128)(2,1)S(1)} %copy-done.4, s32[256]{0:T(256)S(1)} %bitcast.119), kind=kOutput, calls=%fused_computation.2 | convolution fusion | flops 58200576 | bytes 12805120 | tf_op jit(solution)/shard_map/dot_general | solution.py:32
  320.6 5.3 %copy.27 = bf16[256,4,2048]{2,1,0:T(4,128)(2,1)} copy(bf16[256,4,2048]{2,0,1:T(8,128)(2,1)S(1)} %maximum_select_fusion) | data formatting | bytes 8388608
  325.8 5.6 %exponential_reduce_fusion = (f32[256,4,32]{0,2,1:T(8,128)S(1)}, f32[256,4,32]{0,2,1:T(8,128)S(1)}) fusion(s32[256,4,32]{0,2,1:T(8,128)S(1)} %copy-done.22, bf16[32,32,2048,1]{2,1,0,3:T(8,128)(2,1)S(1)} %bitcast.115, bf16[256,4,2048]{2,0,1:T(8,128)(2,1)S(1)} %maximum_select_fusion), kind=kOutput, calls=%fused_computation.9 | convolution fusion | flops 4299096064 | bytes 8781824 | tf_op jit(solution)/shard_map/dot_general | solution.py:90
  (118 shorter events, 29.7 us)
Async XLA Ops:
  7.2 20.6 %copy-start = (f32[256,2048]{1,0:T(8,128)S(1)}, f32[256,2048]{1,0:T(8,128)}, u32[]{:S(2)}) copy-start(f32[256,2048]{1,0:T(8,128)} %param.10) | copy-start | bytes 6291460
  7.2 76.0 %all-gather.8.cloned.1.call-start = ((), (), s32[]{:S(2)}) async-start(), calls=%async_computation.5 | async-start | bytes 4718592 | tf_op jit(solution)/shard_map/all_gather | solution.py:89
  7.9 198.7 %all-gather.4.cloned.1.call-start = ((), (), s32[]{:S(2)}) async-start(), calls=%async_computation.3 | async-start | bytes 14155776 | tf_op jit(solution)/shard_map/all_gather | solution.py:66
  8.7 262.9 %all-gather.6.cloned.1.call-start = ((), (), s32[]{:S(2)}) async-start(), calls=%async_computation.4 | async-start | bytes 7077888 | tf_op jit(solution)/shard_map/all_gather | solution.py:67
  10.8 14.4 %all-to-all-start = ((s32[32,1,8]{2,1,0:T(1,128)}), s32[32,1,8]{2,1,0:T(1,128)S(1)}, u32[]{:S(2)}, u32[]{:S(2)}) async-start(s32[32,1,8]{2,1,0:T(1,128)} %compare_convert_fusion), calls=%async_computation | async-start | bytes 32768 | tf_op jit(solution)/shard_map/all_to_all | solution.py:76
  25.2 10.2 %all-to-all-start.1 = ((s32[32,1,256]{2,1,0:T(1,128)}), s32[32,1,256]{2,1,0:T(1,128)S(1)}, u32[]{:S(2)}, u32[]{:S(2)}) async-start(s32[32,1,256]{2,1,0:T(1,128)} %reshape.433), calls=%async_computation.1 | async-start | bytes 65536 | tf_op jit(solution)/shard_map/all_to_all | solution.py:75
  30.5 7.8 %copy-start.23 = (s32[256,4]{0,1:T(4,128)S(1)}, s32[256,4]{0,1:T(4,128)}, u32[]{:S(2)}) copy-start(s32[256,4]{0,1:T(4,128)} %param.14) | copy-start | bytes 12292
  30.5 7.8 %copy-start.22 = (s32[256,4,32]{0,2,1:T(8,128)S(1)}, s32[256,4,32]{0,2,1:T(8,128)}, u32[]{:S(2)}) copy-start(s32[256,4,32]{0,2,1:T(8,128)} %param.15) | copy-start | bytes 393220
  35.4 189.2 %all-to-all-start.2 = ((f32[32,8,2048]{2,1,0:T(8,128)}), f32[32,8,2048]{2,1,0:T(8,128)S(1)}, u32[]{:S(2)}, u32[]{:S(2)}) async-start(f32[32,8,2048]{2,1,0:T(8,128)} %bitcast.114), calls=%async_computation.2 | async-start | bytes 4194304 | tf_op jit(solution)/shard_map/all_to_all | solution.py:74
  206.6 7.0 %copy-start.3 = (bf16[18,6144]{1,0:T(8,128)(2,1)S(1)}, bf16[18,6144]{1,0:T(8,128)(2,1)}, u32[]{:S(2)}) copy-start(bf16[18,6144]{1,0:T(8,128)(2,1)} %param.18) | copy-start | bytes 663556
  206.6 10.7 %slice-start = ((s8[12582912]{0:T(1024)(128)(4,1)}), s8[4194304]{0:T(1024)(128)(4,1)S(1)}, s32[]{:S(2)}) async-start(s8[12582912]{0:T(1024)(128)(4,1)} %bitcast.103), calls=%async_computation.6 | async-start | bytes 8388608
  206.6 10.7 %slice-start.1 = ((s8[12582912]{0:T(1024)(128)(4,1)}), s8[4194304]{0:T(1024)(128)(4,1)S(1)}, s32[]{:S(2)}) async-start(s8[12582912]{0:T(1024)(128)(4,1)} %bitcast.103), calls=%async_computation.7 | async-start | bytes 8388608
  213.6 3.7 %slice-start.2 = ((s8[12582912]{0:T(1024)(128)(4,1)}), s8[4194304]{0:T(1024)(128)(4,1)S(1)}, s32[]{:S(2)}) async-start(s8[12582912]{0:T(1024)(128)(4,1)} %bitcast.103), calls=%async_computation.8 | async-start | bytes 8388608
  271.6 5.2 %copy-start.2 = (bf16[4,512,1536]{2,1,0:T(8,128)(2,1)S(1)}, bf16[4,512,1536]{2,1,0:T(8,128)(2,1)}, u32[]{:S(2)}) copy-start(bf16[4,512,1536]{2,1,0:T(8,128)(2,1)} %all-gather.6.cloned.1.call-done) | copy-start | bytes 18874372
  274.2 9.1 %slice-start.6 = ((s8[6291456]{0:T(1024)(128)(4,1)}), s8[4194304]{0:T(1024)(128)(4,1)S(1)}, s32[]{:S(2)}) async-start(s8[6291456]{0:T(1024)(128)(4,1)} %bitcast.107), calls=%async_computation.12 | async-start | bytes 8388608
  278.8 4.5 %slice-start.7 = ((s8[6291456]{0:T(1024)(128)(4,1)}), s8[2097152]{0:T(1024)(128)(4,1)S(1)}, s32[]{:S(2)}) async-start(s8[6291456]{0:T(1024)(128)(4,1)} %bitcast.107), calls=%async_computation.13 | async-start | bytes 4194304
  280.9 6.9 %slice-start.3 = ((s8[12582912]{0:T(1024)(128)(4,1)}), s8[4194304]{0:T(1024)(128)(4,1)S(1)}, s32[]{:S(2)}) async-start(s8[12582912]{0:T(1024)(128)(4,1)} %bitcast.105), calls=%async_computation.9 | async-start | bytes 8388608
  281.0 6.9 %slice-start.4 = ((s8[12582912]{0:T(1024)(128)(4,1)}), s8[4194304]{0:T(1024)(128)(4,1)S(1)}, s32[]{:S(2)}) async-start(s8[12582912]{0:T(1024)(128)(4,1)} %bitcast.105), calls=%async_computation.10 | async-start | bytes 8388608
  285.2 2.6 slice-start.5
  287.9 5.6 %copy-start.4 = (bf16[18,6144]{1,0:T(8,128)(2,1)S(1)}, bf16[18,6144]{1,0:T(8,128)(2,1)}, u32[]{:S(2)}) copy-start(bf16[18,6144]{1,0:T(8,128)(2,1)} %param.18) | copy-start | bytes 663556
  293.5 3.9 %copy-start.12 = (f32[256,512]{1,0:T(8,128)S(1)}, f32[256,512]{1,0:T(8,128)}, u32[]{:S(2)}) copy-start(f32[256,512]{1,0:T(8,128)} %get-tuple-element.54) | copy-start | bytes 1572868
  305.7 3.9 %copy-start.10 = (f32[256,512]{1,0:T(8,128)S(1)}, f32[256,512]{1,0:T(8,128)}, u32[]{:S(2)}) copy-start(f32[256,512]{1,0:T(8,128)} %get-tuple-element.27) | copy-start | bytes 1572868
  320.6 5.3 %copy-start.13 = (bf16[1024,2048]{1,0:T(8,128)(2,1)S(1)}, bf16[1024,2048]{1,0:T(8,128)(2,1)}, u32[]{:S(2)}) copy-start(bf16[1024,2048]{1,0:T(8,128)(2,1)} %copy.26) | copy-start | bytes 12582916
  325.8 6.3 %copy-start.1 = (f32[256,2048]{1,0:T(8,128)S(1)}, f32[256,2048]{1,0:T(8,128)}, u32[]{:S(2)}) copy-start(f32[256,2048]{1,0:T(8,128)} %param.10) | copy-start | bytes 6291460
  (14 other events, 16.8 us)
Sparse Core Ops, SparseCore 0:
  9.6 73.5 all-gather.7
  84.8 121.7 all-gather.3
  208.2 63.3 all-gather.5
where the time goes:
time: 339 us
  waiting for transfers between devices  217 us (64%)
  matrix products  59.7 us (18%)
  local copies, waits for them, and re-layouts  20.3 us (6%)
  other arithmetic  15 us (4%)
  between operations  14.3 us (4%)
  starting transfers between devices  12.7 us (4%)
    all_gather x1, waiting for transfers between devices, on_device(): stoch_full = lax.all_gather(w_stoch, 'gy', axis=0, tiled=True)  117 us
    all_gather x1, waiting for transfers between devices, on_device(): deter_full = lax.all_gather(w_deter, 'gy', axis=1, tiled=True)  47 us
    all_gather x1, waiting for transfers between devices, on_device(): prior_full = lax.all_gather(w_prior, 'gy', axis=0, tiled=True)  41.9 us
    dot_general x4, matrix products, imagine(): jnp.dot(onehot, stoch_full, preferred_element_type=jnp.float32)  22.7 us
    dot_general x16, matrix products, imagine(): jnp.dot(before.astype(jnp.bfloat16), deter_full[b], preferred_element_typ...  16.3 us
    dot_general x4, matrix products, imagine(): jnp.dot(act_hot, act_table, preferred_element_type=jnp.float32)  15 us
    unnamed x68, local copies, waits for them, and re-layouts  9.44 us
    concatenate x11, other arithmetic, imagine(): states.append(jnp.concatenate(pieces, 1).astype(jnp.bfloat16))  8.3 us
  transfers between devices with their start and end apart: 6, of which 5 were waited for; matrix products, arithmetic and copies ran while one was open for 10% of the time, Pallas kernels for 0%

commit v1 on v0

--- a/solution.py
+++ b/solution.py
@@ -64,7 +64,7 @@
     slots = peers * cap
     deter = replay_deter.shape[1]
     stoch_full = lax.all_gather(w_stoch, "gy", axis=0, tiled=True)
-    deter_full = lax.all_gather(w_deter, "gy", axis=1, tiled=True)
+    deter_full = jnp.concatenate(lax.all_gather(w_deter, "gy"), axis=1)
     outgoing = (jnp.arange(cap, dtype=jnp.int32)[None, :] < send_counts[0][:, None]).astype(
         jnp.int32
     )

time: 339 us -> 362 us (1.068)
  waiting for transfers between devices: 217 us -> 232 us
  local copies, waits for them, and re-layouts: 20.3 us -> 24.7 us
    all_gather x1, waiting for transfers between devices: 47 us -> 66.1 us  [on_device(): deter_full = jnp.concatenate(lax.all_gather(w_deter, 'gy'), axis=1)]
    slice x0 -> x1, local copies, waits for them, and re-layouts: none -> 5.09 us  [imagine(): deter_full[b]]
    all_gather x1, waiting for transfers between devices: 117 us -> 112 us  [on_device(): stoch_full = lax.all_gather(w_stoch, 'gy', axis=0, tiled=True)]
    unnamed x68 -> x56, local copies, waits for them, and re-layouts: 9.44 us -> 8.74 us
  transfers between devices with their start and end apart: 6 -> 6, of which waited for: 5 -> 5; matrix products, arithmetic and copies ran while one was open for 10% -> 8% of each run, Pallas kernels for 0% -> 0%
where the time goes in v1:
time: 362 us; the launch traced here: 361 us
  waiting for transfers between devices  232 us (64%)
  matrix products  60.2 us (17%)
  local copies, waits for them, and re-layouts  24.7 us (7%)
  other arithmetic  16.2 us (4%)
  between operations  14.3 us (4%)
  starting transfers between devices  13.6 us (4%)
    all_gather x1, waiting for transfers between devices, on_device(): stoch_full = lax.all_gather(w_stoch, 'gy', axis=0, tiled=True)  112 us
    all_gather x1, waiting for transfers between devices, on_device(): deter_full = jnp.concatenate(lax.all_gather(w_deter, 'gy'), axis=1)  66.1 us
    all_gather x1, waiting for transfers between devices, on_device(): prior_full = lax.all_gather(w_prior, 'gy', axis=0, tiled=True)  41.5 us
    dot_general x4, matrix products, imagine(): jnp.dot(onehot, stoch_full, preferred_element_type=jnp.float32)  25.6 us
    dot_general x16, matrix products, imagine(): jnp.dot(before.astype(jnp.bfloat16), deter_full[b], preferred_element_typ...  16.5 us
    dot_general x4, matrix products, imagine(): jnp.dot(act_hot, act_table, preferred_element_type=jnp.float32)  12.3 us
    concatenate x11, other arithmetic, imagine(): states.append(jnp.concatenate(pieces, 1).astype(jnp.bfloat16))  11.1 us
    unnamed x56, local copies, waits for them, and re-layouts  8.74 us
  transfers between devices with their start and end apart: 6, of which 5 were waited for; matrix products, arithmetic and copies ran while one was open for 8% of the time, Pallas kernels for 0%

profile of v1, /device:TPU:0, one launch (start us, length us, event | category | flops | bytes accessed | tf_op | source)
XLA Modules:
  0.0 361.0 jit_solution(18183628347344249325)
XLA Ops:
  10.1 7.3 %all-to-all-start = ((s32[32,1,8]{2,1,0:T(1,128)}), s32[32,1,8]{2,1,0:T(1,128)S(1)}, u32[]{:S(2)}, u32[]{:S(2)}) async-start(s32[32,1,8]{2,1,0:T(1,128)} %compare_convert_fusion), calls=%async_computation | async-start | bytes 32768 | tf_op jit(solution)/shard_map/all_to_all | solution.py:76
  19.3 5.3 %all-to-all-done = s32[32,1,8]{2,1,0:T(1,128)S(1)} async-done(((s32[32,1,8]{2,1,0:T(1,128)}), s32[32,1,8]{2,1,0:T(1,128)S(1)}, u32[]{:S(2)}, u32[]{:S(2)}) %all-to-all-start) | async-done | bytes 1056 | tf_op jit(solution)/shard_map/all_to_all | solution.py:76
  24.6 2.6 all-to-all-start.1
  27.2 2.7 gather_fusion.1
  29.8 5.0 %all-to-all-done.1 = s32[32,1,256]{2,1,0:T(1,128)S(1)} async-done(((s32[32,1,256]{2,1,0:T(1,128)}), s32[32,1,256]{2,1,0:T(1,128)S(1)}, u32[]{:S(2)}, u32[]{:S(2)}) %all-to-all-start.1) | async-done | bytes 32800 | tf_op jit(solution)/shard_map/all_to_all | solution.py:75
  34.8 3.6 all-to-all-start.2
  41.6 41.5 %all-gather.7.cloned.1.call-done = bf16[2048,1024]{1,0:T(8,128)(2,1)} async-done(((bf16[256,1024]{1,0:T(8,128)(2,1)}), bf16[2048,1024]{1,0:T(8,128)(2,1)}) %all-gather.7.cloned.1.call-update) | async-done | bytes 4194320 | tf_op jit(solution)/shard_map/all_gather | solution.py:89
  83.1 6.6 %copy.26 = bf16[1024,2048]{1,0:T(8,128)(2,1)} copy(bf16[1024,2048]{0,1:T(8,128)(2,1)} %bitcast.123) | data formatting | bytes 8388608 | tf_op jit(solution)/shard_map/dot_general | solution.py:90
  89.7 66.1 %all-gather.9.cloned.1.call-done = bf16[32,64,1536]{2,1,0:T(8,128)(2,1)} async-done(((bf16[4,64,1536]{2,1,0:T(8,128)(2,1)}), bf16[32,64,1536]{2,1,0:T(8,128)(2,1)}) %all-gather.9.cloned.1.call-update) | async-done | bytes 6291472 | tf_op jit(solution)/shard_map/all_gather | solution.py:67
  155.8 5.1 %fusion.198 = (bf16[1,8,64,1536]{3,2,0,1:T(8,128)(2,1)}, bf16[1,8,64,1536]{3,2,0,1:T(8,128)(2,1)S(1)}, bf16[1,8,64,1536]{3,2,0,1:T(8,128)(2,1)}, bf16[1,8,64,1536]{3,2,0,1:T(8,128)(2,1)}) fusion(bf16[4,8,64,1536]{3,2,0,1:T(8,128)(2,1)} %bitcast.121), kind=kLoop, calls=%fused_computation.292 | loop fusion | bytes 12582912 | tf_op jit(solution)/shard_map/slice | solution.py:39
  160.9 111.9 %all-gather.5.cloned.1.call-done = bf16[1024,6144]{1,0:T(8,128)(2,1)} async-done(((bf16[128,6144]{1,0:T(8,128)(2,1)}), bf16[1024,6144]{1,0:T(8,128)(2,1)}) %all-gather.5.cloned.1.call-update) | async-done | bytes 12582928 | tf_op jit(solution)/shard_map/all_gather | solution.py:66
  272.8 6.7 %fusion.200 = f32[256,6144]{1,0:T(8,128)S(1)} fusion(pred[256,1024]{0,1:T(32,128)(4,1)S(1)} %get-tuple-element.54, bf16[1024,6144]{1,0:T(8,128)(2,1)} %all-gather.5.cloned.1.call-done), kind=kOutput, calls=%fused_computation.294 | convolution fusion | flops 3221225472 | bytes 19136512 | tf_op jit(solution)/shard_map/dot_general | solution.py:32
  279.6 3.7 %convolution_add_fusion.3 = f32[256,6144]{1,0:T(8,128)} fusion(f32[256,6144]{1,0:T(8,128)S(1)} %fusion.200, bf16[18,6144]{1,0:T(8,128)(2,1)S(1)} %copy-done.6, s32[256]{0:T(256)S(1)} %bitcast.129), kind=kOutput, calls=%fused_computation.5 | convolution fusion | flops 58200576 | bytes 12805120 | tf_op jit(solution)/shard_map/dot_general | solution.py:32
  283.3 2.3 convolution_add_fusion.16
  285.6 2.7 convolution_add_fusion.17
  290.2 2.8 convolution_add_fusion.19
  293.0 6.7 %fusion.201 = f32[256,6144]{1,0:T(8,128)S(1)} fusion(pred[256,1024]{0,1:T(32,128)(4,1)S(1)} %get-tuple-element.52, bf16[1024,6144]{1,0:T(8,128)(2,1)} %all-gather.5.cloned.1.call-done), kind=kOutput, calls=%fused_computation.295 | convolution fusion | flops 3221225472 | bytes 19136512 | tf_op jit(solution)/shard_map/dot_general | solution.py:32
  300.7 4.4 %convert_bitcast_fusion.11 = (bf16[256,1,512]{2,0,1:T(8,128)(2,1)}, f32[256,512]{1,0:T(8,128)S(1)}, bf16[256,1,512]{2,0,1:T(8,128)(2,1)}, f32[256,512]{1,0:T(8,1...) fusion(f32[256,2048]{1,0:T(8,128)} %bitcast.6, ...), kind=kLoop, calls=%fused_computation.279 | loop fusion | flops 6815744 | bytes 11534336 | tf_op jit(solution)/shard_map/concatenate | solution.py:46
  308.4 5.6 %fusion.202 = f32[256,6144]{1,0:T(8,128)} fusion(pred[256,1024]{0,1:T(32,128)(4,1)S(1)} %copy-done.10, bf16[1024,6144]{1,0:T(8,128)(2,1)S(1)} %bitcast.103), kind=kOutput, calls=%fused_computation.296 | convolution fusion | flops 3221225472 | bytes 19136512 | tf_op jit(solution)/shard_map/dot_general | solution.py:32
  314.0 3.8 %convolution_add_fusion.1 = f32[256,6144]{1,0:T(8,128)S(1)} fusion(f32[256,6144]{1,0:T(8,128)} %fusion.202, bf16[18,6144]{1,0:T(8,128)(2,1)S(1)} %copy-done.6, s32[256]{0:T(256)S(1)} %bitcast.127), kind=kOutput, calls=%fused_computation.3 | convolution fusion | flops 58200576 | bytes 12805120 | tf_op jit(solution)/shard_map/dot_general | solution.py:32
  320.5 6.6 %fusion.203 = f32[256,6144]{1,0:T(8,128)} fusion(pred[256,1024]{0,1:T(32,128)(4,1)} %get-tuple-element.51, bf16[1024,6144]{1,0:T(8,128)(2,1)S(1)} %bitcast.103), kind=kOutput, calls=%fused_computation.297 | convolution fusion | flops 3221225472 | bytes 19136512 | tf_op jit(solution)/shard_map/dot_general | solution.py:32
  327.1 3.8 %convolution_add_fusion = f32[256,6144]{1,0:T(8,128)S(1)} fusion(f32[256,6144]{1,0:T(8,128)} %fusion.203, bf16[18,6144]{1,0:T(8,128)(2,1)S(1)} %copy-done.6, s32[256]{0:T(256)S(1)} %bitcast.126), kind=kOutput, calls=%fused_computation.2 | convolution fusion | flops 58200576 | bytes 12805120 | tf_op jit(solution)/shard_map/dot_general | solution.py:32
  342.7 5.3 %copy.27 = bf16[256,4,2048]{2,1,0:T(4,128)(2,1)} copy(bf16[256,4,2048]{2,0,1:T(8,128)(2,1)S(1)} %maximum_select_fusion) | data formatting | bytes 8388608
  347.9 5.8 %exponential_reduce_fusion = (f32[256,4,32]{0,2,1:T(8,128)S(1)}, f32[256,4,32]{0,2,1:T(8,128)S(1)}) fusion(s32[256,4,32]{0,2,1:T(8,128)S(1)} %copy-done.18, bf16[32,32,2048,1]{2,1,0,3:T(8,128)(2,1)S(1)} %bitcast.122, bf16[256,4,2048]{2,0,1:T(8,128)(2,1)S(1)} %maximum_select_fusion), kind=kOutput, calls=%fused_computation.9 | convolution fusion | flops 4299096064 | bytes 8781824 | tf_op jit(solution)/shard_map/dot_general | solution.py:90
  (105 shorter events, 28.8 us)
Async XLA Ops:
  7.2 20.0 %copy-start = (f32[256,2048]{1,0:T(8,128)S(1)}, f32[256,2048]{1,0:T(8,128)}, u32[]{:S(2)}) copy-start(f32[256,2048]{1,0:T(8,128)} %param.10) | copy-start | bytes 6291460
  7.2 2.3 copy-start.22
  7.2 10.3 %copy-start.20 = (s32[32,8]{0,1:T(8,128)S(1)}, s32[32,8]{0,1:T(8,128)}, u32[]{:S(2)}) copy-start(s32[32,8]{0,1:T(8,128)} %param.12) | copy-start | bytes 3076
  7.2 10.5 %copy-start.19 = (s32[256,32]{0,1:T(8,128)S(1)}, s32[256,32]{0,1:T(8,128)}, u32[]{:S(2)}) copy-start(s32[256,32]{0,1:T(8,128)} %param.11) | copy-start | bytes 98308
  7.2 75.9 %all-gather.7.cloned.1.call-start = ((), (), s32[]{:S(2)}) async-start(), calls=%async_computation.4 | async-start | bytes 4718592 | tf_op jit(solution)/shard_map/all_gather | solution.py:89
  7.9 147.9 %all-gather.9.cloned.1.call-start = ((), (), s32[]{:S(2)}) async-start(), calls=%async_computation.5 | async-start | bytes 7077888 | tf_op jit(solution)/shard_map/all_gather | solution.py:67
  8.7 264.1 %all-gather.5.cloned.1.call-start = ((), (), s32[]{:S(2)}) async-start(), calls=%async_computation.3 | async-start | bytes 14155776 | tf_op jit(solution)/shard_map/all_gather | solution.py:66
  10.1 14.4 %all-to-all-start = ((s32[32,1,8]{2,1,0:T(1,128)}), s32[32,1,8]{2,1,0:T(1,128)S(1)}, u32[]{:S(2)}, u32[]{:S(2)}) async-start(s32[32,1,8]{2,1,0:T(1,128)} %compare_convert_fusion), calls=%async_computation | async-start | bytes 32768 | tf_op jit(solution)/shard_map/all_to_all | solution.py:76
  24.6 10.2 %all-to-all-start.1 = ((s32[32,1,256]{2,1,0:T(1,128)}), s32[32,1,256]{2,1,0:T(1,128)S(1)}, u32[]{:S(2)}, u32[]{:S(2)}) async-start(s32[32,1,256]{2,1,0:T(1,128)} %reshape.447), calls=%async_computation.1 | async-start | bytes 65536 | tf_op jit(solution)/shard_map/all_to_all | solution.py:75
  34.8 3.7 %copy-start.21 = (s32[256,4]{0,1:T(4,128)S(1)}, s32[256,4]{0,1:T(4,128)}, u32[]{:S(2)}) copy-start(s32[256,4]{0,1:T(4,128)} %param.14) | copy-start | bytes 12292
  34.8 3.7 %copy-start.18 = (s32[256,4,32]{0,2,1:T(8,128)S(1)}, s32[256,4,32]{0,2,1:T(8,128)}, u32[]{:S(2)}) copy-start(s32[256,4,32]{0,2,1:T(8,128)} %param.15) | copy-start | bytes 393220
  34.8 248.5 %all-to-all-start.2 = ((f32[32,8,2048]{2,1,0:T(8,128)}), f32[32,8,2048]{2,1,0:T(8,128)}, u32[]{:S(2)}, u32[]{:S(2)}) async-start(f32[32,8,2048]{2,1,0:T(8,128)} %bitcast.120), calls=%async_computation.2 | async-start | bytes 4194304 | tf_op jit(solution)/shard_map/all_to_all | solution.py:74
  272.8 6.7 %copy-start.6 = (bf16[18,6144]{1,0:T(8,128)(2,1)S(1)}, bf16[18,6144]{1,0:T(8,128)(2,1)}, u32[]{:S(2)}) copy-start(bf16[18,6144]{1,0:T(8,128)(2,1)} %param.18) | copy-start | bytes 663556
  283.3 2.3 copy-start.2
  283.3 5.1 %copy-start.5 = (f32[256,6144]{1,0:T(8,128)S(1)}, f32[256,6144]{1,0:T(8,128)}, u32[]{:S(2)}) copy-start(f32[256,6144]{1,0:T(8,128)} %convolution_add_fusion.3) | copy-start | bytes 18874372
  285.6 2.9 copy-start.3
  288.5 1.7 copy-start.4
  300.7 7.0 %slice-start = ((s8[12582912]{0:T(1024)(128)(4,1)}), s8[4194304]{0:T(1024)(128)(4,1)S(1)}, s32[]{:S(2)}) async-start(s8[12582912]{0:T(1024)(128)(4,1)} %bitcast.102), calls=%async_computation.6 | async-start | bytes 8388608
  300.7 7.0 %slice-start.1 = ((s8[12582912]{0:T(1024)(128)(4,1)}), s8[4194304]{0:T(1024)(128)(4,1)S(1)}, s32[]{:S(2)}) async-start(s8[12582912]{0:T(1024)(128)(4,1)} %bitcast.102), calls=%async_computation.7 | async-start | bytes 8388608
  305.6 2.6 slice-start.2
  306.2 2.1 copy-start.10
  307.6 10.2 %copy-start.8 = (f32[256,512]{1,0:T(8,128)}, f32[256,512]{1,0:T(8,128)S(1)}, u32[]{:S(2)}) copy-start(f32[256,512]{1,0:T(8,128)S(1)} %get-tuple-element.58) | copy-start | bytes 1572868
  342.7 5.3 %copy-start.9 = (bf16[1024,2048]{1,0:T(8,128)(2,1)S(1)}, bf16[1024,2048]{1,0:T(8,128)(2,1)}, u32[]{:S(2)}) copy-start(bf16[1024,2048]{1,0:T(8,128)(2,1)} %copy.26) | copy-start | bytes 12582916
  347.9 6.5 %copy-start.1 = (f32[256,2048]{1,0:T(8,128)S(1)}, f32[256,2048]{1,0:T(8,128)}, u32[]{:S(2)}) copy-start(f32[256,2048]{1,0:T(8,128)} %param.10) | copy-start | bytes 6291460
  (8 other events, 9.2 us)
Sparse Core Ops, SparseCore 0:
  9.6 73.4 all-gather.6
  84.8 71.0 all-gather.8
  157.4 115.3 all-gather.4
